TPU v7x, 32 devices: a whole 2x2x4 slice. The times are simulated.
32 devices in a mesh: leaf: 8 (over z, core), grp: 4 (over y, x).
Axes of the slice: x: 2, y: 2, z: 4, core: 2. Of those that a mesh axis runs over, the one named last changes fastest.
Arguments:
- front_rows: bfloat16 [8192, 6144], P('leaf', 'grp'), may hold values from -0.078125 to 0.078125
- sample_matrix: bfloat16 [6144, 1024], P('grp'), may hold values from -6 to 6
- pivots: int32 [15, 512], replicated, may hold values from 0 to 1023, as said below
Outputs:
- bases: float32 [4, 8, 1024, 512], P(None, 'leaf', 'grp')
- top_sample: float32 [1024, 512], P('grp')
Inputs may be any that keep to these rules, and one draw needn't show every extreme that they name: `pivots`: row o_l + j (o_l = 2 * 8 - 2 * 8 / 2^l) holds node j of level l: 512 distinct column numbers of its 1024 columns; entries k * 128 to (k + 1) * 128 - 1 lie in k * 256 to (k + 1) * 256 - 1.
All inputs are finite; a program needn't handle non-finite values.
Results may differ from a plain program's by a relative error of at most 0.0003.
Values sent between devices are 32-bit elements; how exact they have to be, the bound alone decides.
A program may use at most 128 MiB of HBM per device.

v0:
```python
import jax
import jax.numpy as jnp
from jax import lax
from jax.sharding import PartitionSpec as P


def from_partner(x, axis, bit):
    return lax.ppermute(x, axis, [(i, i ^ 1 << bit) for i in range(lax.axis_size(axis))])


def contract_last(left_side, right_side):
    return lax.dot_general(
        left_side,
        right_side,
        (((1,), (1,)), ((), ())),
        precision=lax.Precision.HIGHEST,
        preferred_element_type=jnp.float32,
    )


def basis_from(gram, cross):
    factor = jnp.linalg.cholesky(gram)
    identity = jnp.eye(gram.shape[0], dtype=gram.dtype)
    inverse_factor = jax.scipy.linalg.solve_triangular(factor, identity, lower=True)
    gram_inverse = jnp.dot(
        inverse_factor.T,
        inverse_factor,
        precision=lax.Precision.HIGHEST,
        preferred_element_type=jnp.float32,
    )
    return jnp.dot(
        cross, gram_inverse, precision=lax.Precision.HIGHEST, preferred_element_type=jnp.float32
    )


def on_device(front_rows, sample_matrix, pivots):
    leaf_count = lax.axis_size("leaf")
    grp_count = lax.axis_size("grp")
    merges = leaf_count.bit_length() - 1
    leaf_index = lax.axis_index("leaf")
    grp_index = lax.axis_index("grp")
    node_rows = front_rows.shape[0]
    rank_size = pivots.shape[1]
    cols_dev = sample_matrix.shape[1] // grp_count
    rows_dev = node_rows // grp_count
    piv_dev = rank_size // grp_count
    collected = []
    row_block = lax.psum_scatter(
        jnp.dot(front_rows, sample_matrix, preferred_element_type=jnp.float32),
        "grp",
        scatter_dimension=0,
        tiled=True,
    )
    half_count = grp_count // 2
    wanted_side = (grp_index >= half_count).astype(jnp.int32)
    skeleton_t = row_block
    for depth_level in range(merges + 1):
        offset = 2 * leaf_count - (2 * leaf_count >> depth_level)
        node_index = offset + (leaf_index >> depth_level)
        chosen = lax.dynamic_index_in_dim(pivots, node_index, 0, keepdims=False)
        local_picks = (
            lax.dynamic_slice_in_dim(chosen, grp_index * piv_dev, piv_dev) - grp_index * rows_dev
        )
        picked = jnp.take(row_block, local_picks, axis=0)
        skeleton_t = lax.all_gather(picked, "grp", axis=0, tiled=True)
        gram = contract_last(skeleton_t, skeleton_t)
        cross = contract_last(row_block, skeleton_t)
        collected.append(basis_from(gram, cross))
        if depth_level < merges:
            piece = lax.dynamic_slice_in_dim(
                skeleton_t, grp_index % half_count * rows_dev, rows_dev, 0
            )
            partner = from_partner(piece, "leaf", depth_level)
            which_side = (leaf_index >> depth_level) % 2
            row_block = jnp.where(which_side == wanted_side, piece, partner)
    skeleton = lax.dynamic_slice_in_dim(skeleton_t, grp_index * cols_dev, cols_dev, 1).T
    return (jnp.stack(collected)[:, None], skeleton)


def solution(mesh):
    placed = (P("leaf", "grp"), P("grp", None), P())
    return jax.shard_map(
        on_device,
        mesh=mesh,
        in_specs=placed,
        out_specs=(P(None, "leaf", "grp", None), P("grp", None)),
        check_vma=False,
    )
```

profile of v0, /device:TPU:0, one launch (start us, length us, event | category | flops | bytes accessed | tf_op | source)
XLA Modules:
  0.0 843.9 jit_solution(6618450672089239020)
XLA Ops:
  9.1 6.8 fusion.161
  16.9 54.5 %reduce-scatter.2.cloned.1.call-done = f32[256,1024]{1,0:T(8,128)} async-done(((f32[1024,1024]{1,0:T(8,128)}), f32[256,1024]{1,0:T(8,128)}) %reduce-scatter.2.cloned.1.call-update) | async-done | bytes 1048592 | tf_op jit(solution)/shard_map/reduce_scatter | solution.py:48
  75.8 34.1 %all-gather.5.cloned.1.call-done = f32[512,1024]{1,0:T(8,128)} async-done(((f32[128,1024]{1,0:T(8,128)}), f32[512,1024]{1,0:T(8,128)}) %all-gather.5.cloned.1.call-update) | async-done | bytes 2097168 | tf_op jit(solution)/shard_map/all_gather | solution.py:65
  109.8 5.7 fusion.163
  117.1 11.7 %cholesky.462 = f32[128,128]{1,0:T(8,128)S(1)} custom-call(f32[128,128]{1,0:T(8,128)S(1)} %cholesky.746), custom_call_target="Cholesky" | custom-call | tf_op jit(solution)/shard_map/jit(cholesky)/cholesky | solution.py:22
  128.9 9.8 %custom-call.35 = f32[1,128,128]{1,2,0:T(8,128)S(1)} custom-call(f32[1,128,128]{2,1,0:T(8,128)S(1)} %get-tuple-element.94), custom_call_target="InvertDiagBlocksLowerTriangular" | custom-call | tf_op jit(solution)/shard_map/jit(cholesky)/cholesky | solution.py:22
  141.4 20.5 %cholesky.481 = f32[128,128]{1,0:T(8,128)S(1)} custom-call(f32[128,128]{1,0:T(8,128)S(1)} %cholesky.750), custom_call_target="Cholesky" | custom-call | tf_op jit(solution)/shard_map/jit(cholesky)/cholesky | solution.py:22
  161.9 9.8 %custom-call.36 = f32[1,128,128]{1,2,0:T(8,128)S(1)} custom-call(f32[1,128,128]{2,1,0:T(8,128)S(1)} %get-tuple-element.91), custom_call_target="InvertDiagBlocksLowerTriangular" | custom-call | tf_op jit(solution)/shard_map/jit(cholesky)/cholesky | solution.py:22
  173.2 11.7 %cholesky.502 = f32[128,128]{1,0:T(8,128)S(1)} custom-call(f32[128,128]{1,0:T(8,128)S(1)} %cholesky.755), custom_call_target="Cholesky" | custom-call | tf_op jit(solution)/shard_map/jit(cholesky)/cholesky | solution.py:22
  185.0 9.8 %custom-call.37 = f32[1,128,128]{1,2,0:T(8,128)S(1)} custom-call(f32[1,128,128]{2,1,0:T(8,128)S(1)} %get-tuple-element.88), custom_call_target="InvertDiagBlocksLowerTriangular" | custom-call | tf_op jit(solution)/shard_map/jit(cholesky)/cholesky | solution.py:22
  197.6 11.7 %cholesky.519 = f32[128,128]{1,0:T(8,128)S(1)} custom-call(f32[128,128]{1,0:T(8,128)S(1)} %convolution_subtract_fusion.23), custom_call_target="Cholesky" | custom-call | tf_op jit(solution)/shard_map/jit(cholesky)/cholesky | solution.py:22
  219.5 14.1 %while.8 = (s32[]{:T(128)}, f32[512,512]{1,0:T(8,128)}, s32[4,2]{0,1:T(2,128)S(1)}, f32[4,128,128]{2,1,0:T(8,128)}, s32[]{:T(128)}) while((s32[]{:T(128)}, f32[512,512]{1,0:T(8,128)}, s32[4,2]{0,1:T(2,128)S(1)}, f32[4,128,128]{2,1,0:T(8,128)}, s32[]{:T(128)}) %tuple.121), condition=%wide.while_cond, body=%wide.while_body.sunk | while | flops 2 | bytes 132205 | solution.py:24
  227.2 2.9 bitcast_dynamic-update-slice_fusion.8
  233.6 41.1 %custom-call.38 = f32[4,128,128]{1,2,0:T(8,128)} custom-call(f32[4,128,128]{2,1,0:T(8,128)} %get-tuple-element.31), custom_call_target="InvertDiagBlocksLowerTriangular" | custom-call | tf_op jit(solution)/shard_map/jit(_solve_triangular)/triangular_solve | solution.py:24
  288.5 5.7 fusion.165
  295.8 11.9 %cholesky.534 = f32[128,128]{1,0:T(8,128)S(1)} custom-call(f32[128,128]{1,0:T(8,128)S(1)} %cholesky.759), custom_call_target="Cholesky" | custom-call | tf_op jit(solution)/shard_map/jit(cholesky)/cholesky | solution.py:22
  307.7 9.8 %custom-call.39 = f32[1,128,128]{1,2,0:T(8,128)S(1)} custom-call(f32[1,128,128]{2,1,0:T(8,128)S(1)} %get-tuple-element.104), custom_call_target="InvertDiagBlocksLowerTriangular" | custom-call | tf_op jit(solution)/shard_map/jit(cholesky)/cholesky | solution.py:22
  321.9 11.7 %cholesky.553 = f32[128,128]{1,0:T(8,128)S(1)} custom-call(f32[128,128]{1,0:T(8,128)S(1)} %cholesky.763), custom_call_target="Cholesky" | custom-call | tf_op jit(solution)/shard_map/jit(cholesky)/cholesky | solution.py:22
  334.2 10.2 %custom-call.40 = f32[1,128,128]{1,2,0:T(8,128)S(1)} custom-call(f32[1,128,128]{2,1,0:T(8,128)S(1)} %get-tuple-element.101), custom_call_target="InvertDiagBlocksLowerTriangular" | custom-call | tf_op jit(solution)/shard_map/jit(cholesky)/cholesky | solution.py:22
  346.8 11.7 %cholesky.574 = f32[128,128]{1,0:T(8,128)S(1)} custom-call(f32[128,128]{1,0:T(8,128)S(1)} %cholesky.768), custom_call_target="Cholesky" | custom-call | tf_op jit(solution)/shard_map/jit(cholesky)/cholesky | solution.py:22
  359.2 9.8 %custom-call.41 = f32[1,128,128]{1,2,0:T(8,128)S(1)} custom-call(f32[1,128,128]{2,1,0:T(8,128)S(1)} %get-tuple-element.98), custom_call_target="InvertDiagBlocksLowerTriangular" | custom-call | tf_op jit(solution)/shard_map/jit(cholesky)/cholesky | solution.py:22
  373.9 11.7 %cholesky.591 = f32[128,128]{1,0:T(8,128)S(1)} custom-call(f32[128,128]{1,0:T(8,128)S(1)} %convolution_subtract_fusion.22), custom_call_target="Cholesky" | custom-call | tf_op jit(solution)/shard_map/jit(cholesky)/cholesky | solution.py:22
  400.1 13.8 %while.9 = (s32[]{:T(128)}, f32[512,512]{1,0:T(8,128)}, s32[4,2]{0,1:T(2,128)S(1)}, f32[4,128,128]{2,1,0:T(8,128)}, s32[]{:T(128)}) while((s32[]{:T(128)}, f32[512,512]{1,0:T(8,128)}, s32[4,2]{0,1:T(2,128)S(1)}, f32[4,128,128]{2,1,0:T(8,128)}, s32[]{:T(128)}) %tuple.134), condition=%wide.while_cond.clone, body=%wide.while_body.clone.sunk | while | flops 2 | bytes 132205 | solution.py:24
  413.9 40.9 %custom-call.42 = f32[4,128,128]{1,2,0:T(8,128)} custom-call(f32[4,128,128]{2,1,0:T(8,128)} %get-tuple-element.32), custom_call_target="InvertDiagBlocksLowerTriangular" | custom-call | tf_op jit(solution)/shard_map/jit(_solve_triangular)/triangular_solve | solution.py:24
  468.3 5.7 fusion.167
  477.9 12.1 %cholesky.606 = f32[128,128]{1,0:T(8,128)S(1)} custom-call(f32[128,128]{1,0:T(8,128)S(1)} %cholesky.772), custom_call_target="Cholesky" | custom-call | tf_op jit(solution)/shard_map/jit(cholesky)/cholesky | solution.py:22
  490.0 9.8 %custom-call.43 = f32[1,128,128]{1,2,0:T(8,128)S(1)} custom-call(f32[1,128,128]{2,1,0:T(8,128)S(1)} %get-tuple-element.114), custom_call_target="InvertDiagBlocksLowerTriangular" | custom-call | tf_op jit(solution)/shard_map/jit(cholesky)/cholesky | solution.py:22
  502.5 11.7 %cholesky.625 = f32[128,128]{1,0:T(8,128)S(1)} custom-call(f32[128,128]{1,0:T(8,128)S(1)} %cholesky.776), custom_call_target="Cholesky" | custom-call | tf_op jit(solution)/shard_map/jit(cholesky)/cholesky | solution.py:22
  514.2 10.0 %custom-call.44 = f32[1,128,128]{1,2,0:T(8,128)S(1)} custom-call(f32[1,128,128]{2,1,0:T(8,128)S(1)} %get-tuple-element.111), custom_call_target="InvertDiagBlocksLowerTriangular" | custom-call | tf_op jit(solution)/shard_map/jit(cholesky)/cholesky | solution.py:22
  525.8 11.7 %cholesky.646 = f32[128,128]{1,0:T(8,128)S(1)} custom-call(f32[128,128]{1,0:T(8,128)S(1)} %cholesky.781), custom_call_target="Cholesky" | custom-call | tf_op jit(solution)/shard_map/jit(cholesky)/cholesky | solution.py:22
  537.5 9.8 %custom-call.45 = f32[1,128,128]{1,2,0:T(8,128)S(1)} custom-call(f32[1,128,128]{2,1,0:T(8,128)S(1)} %get-tuple-element.108), custom_call_target="InvertDiagBlocksLowerTriangular" | custom-call | tf_op jit(solution)/shard_map/jit(cholesky)/cholesky | solution.py:22
  553.5 11.7 %cholesky.663 = f32[128,128]{1,0:T(8,128)S(1)} custom-call(f32[128,128]{1,0:T(8,128)S(1)} %convolution_subtract_fusion.21), custom_call_target="Cholesky" | custom-call | tf_op jit(solution)/shard_map/jit(cholesky)/cholesky | solution.py:22
  571.0 28.0 %collective-permute-done.2 = f32[256,1024]{1,0:T(8,128)} collective-permute-done((f32[256,1024]{1,0:T(8,128)}, f32[256,1024]{1,0:T(8,128)}, u32[]{:S(2)}, u32[]{:S(2)}) %collective-permute-start.2) | collective-permute-done | bytes 1048608 | tf_op jit(solution)/shard_map/ppermute | solution.py:8
  604.7 14.2 %while.10 = (s32[]{:T(128)}, f32[512,512]{1,0:T(8,128)}, s32[4,2]{0,1:T(2,128)S(1)}, f32[4,128,128]{2,1,0:T(8,128)}, s32[]{:T(128)}) while((s32[]{:T(128)}, f32[512,512]{1,0:T(8,128)}, s32[4,2]{0,1:T(2,128)S(1)}, f32[4,128,128]{2,1,0:T(8,128)}, s32[]{:T(128)}) %tuple.135), condition=%wide.while_cond.clone.1, body=%wide.while_body.clone.1.sunk | while | flops 2 | bytes 132205 | solution.py:24
  605.3 2.9 bitcast_dynamic-update-slice_fusion.10
  608.9 2.9 bitcast_dynamic-update-slice_fusion.10
  612.5 2.9 bitcast_dynamic-update-slice_fusion.10
  618.8 41.1 %custom-call.46 = f32[4,128,128]{1,2,0:T(8,128)} custom-call(f32[4,128,128]{2,1,0:T(8,128)} %get-tuple-element.33), custom_call_target="InvertDiagBlocksLowerTriangular" | custom-call | tf_op jit(solution)/shard_map/jit(_solve_triangular)/triangular_solve | solution.py:24
  675.5 5.7 fusion.169
  685.0 11.9 %cholesky.678 = f32[128,128]{1,0:T(8,128)S(1)} custom-call(f32[128,128]{1,0:T(8,128)S(1)} %cholesky.785), custom_call_target="Cholesky" | custom-call | tf_op jit(solution)/shard_map/jit(cholesky)/cholesky | solution.py:22
  696.9 9.8 %custom-call.47 = f32[1,128,128]{1,2,0:T(8,128)S(1)} custom-call(f32[1,128,128]{2,1,0:T(8,128)S(1)} %get-tuple-element.124), custom_call_target="InvertDiagBlocksLowerTriangular" | custom-call | tf_op jit(solution)/shard_map/jit(cholesky)/cholesky | solution.py:22
  709.4 11.7 %cholesky.697 = f32[128,128]{1,0:T(8,128)S(1)} custom-call(f32[128,128]{1,0:T(8,128)S(1)} %cholesky.789), custom_call_target="Cholesky" | custom-call | tf_op jit(solution)/shard_map/jit(cholesky)/cholesky | solution.py:22
  721.1 10.0 %custom-call.48 = f32[1,128,128]{1,2,0:T(8,128)S(1)} custom-call(f32[1,128,128]{2,1,0:T(8,128)S(1)} %get-tuple-element.121), custom_call_target="InvertDiagBlocksLowerTriangular" | custom-call | tf_op jit(solution)/shard_map/jit(cholesky)/cholesky | solution.py:22
  732.7 11.7 %cholesky.718 = f32[128,128]{1,0:T(8,128)S(1)} custom-call(f32[128,128]{1,0:T(8,128)S(1)} %cholesky.794), custom_call_target="Cholesky" | custom-call | tf_op jit(solution)/shard_map/jit(cholesky)/cholesky | solution.py:22
  745.2 9.8 %custom-call.49 = f32[1,128,128]{1,2,0:T(8,128)S(1)} custom-call(f32[1,128,128]{2,1,0:T(8,128)S(1)} %get-tuple-element.118), custom_call_target="InvertDiagBlocksLowerTriangular" | custom-call | tf_op jit(solution)/shard_map/jit(cholesky)/cholesky | solution.py:22
  756.4 11.7 %cholesky.735 = f32[128,128]{1,0:T(8,128)S(1)} custom-call(f32[128,128]{1,0:T(8,128)S(1)} %convolution_subtract_fusion.20), custom_call_target="Cholesky" | custom-call | tf_op jit(solution)/shard_map/jit(cholesky)/cholesky | solution.py:22
  773.2 11.7 %while.11 = (s32[]{:T(128)}, f32[512,512]{1,0:T(8,128)}, s32[4,2]{0,1:T(2,128)S(1)}, f32[4,128,128]{2,1,0:T(8,128)S(1)}, s32[]{:T(128)}) while((s32[]{:T(128)}, f32[512,512]{1,0:T(8,128)}, s32[4,2]{0,1:T(2,128)S(1)}, f32[4,128,128]{2,1,0:T(8,128)S(1)}, s32[]{:T(128)}) %tuple.136), condition=%wide.while_cond.clone.2, body=%wide.while_body.clone.2.sunk | while | flops 2 | bytes 131189 | solution.py:24
  784.9 39.6 %custom-call.50 = f32[4,128,128]{1,2,0:T(8,128)S(1)} custom-call(f32[4,128,128]{2,1,0:T(8,128)S(1)} %get-tuple-element.34), custom_call_target="InvertDiagBlocksLowerTriangular" | custom-call | tf_op jit(solution)/shard_map/jit(_solve_triangular)/triangular_solve | solution.py:24
  (253 shorter events, 182.2 us)
Async XLA Ops:
  7.2 1.9 copy-start
  7.2 64.2 %reduce-scatter.2.cloned.1.call-start = ((), (), s32[]{:S(2)}) async-start(), calls=%async_computation.1 | async-start | bytes 5242880 | tf_op jit(solution)/shard_map/reduce_scatter | solution.py:48
  15.9 94.0 %all-gather.5.cloned.1.call-start = ((), (), s32[]{:S(2)}) async-start(), calls=%async_computation.2 | async-start | bytes 2621440 | tf_op jit(solution)/shard_map/all_gather | solution.py:65
  74.5 214.0 %all-gather.7.cloned.1.call-start = ((), (), s32[]{:S(2)}) async-start(), calls=%async_computation.3 | async-start | bytes 2621440 | tf_op jit(solution)/shard_map/all_gather | solution.py:65
  116.2 1.0 copy-start.11
  128.9 66.0 %copy-start.2 = (f32[512,1024]{1,0:T(8,128)S(1)}, f32[512,1024]{1,0:T(8,128)}, u32[]{:S(2)}) copy-start(f32[512,1024]{1,0:T(8,128)} %all-gather.5.cloned.1.call-done) | copy-start | bytes 6291460
  195.9 19.1 %collective-permute-start = (f32[256,1024]{1,0:T(8,128)}, f32[256,1024]{1,0:T(8,128)}, u32[]{:S(2)}, u32[]{:S(2)}) collective-permute-start(f32[256,1024]{1,0:T(8,128)} %constant_dynamic-slice_fusion.6), channel_id=1, source_target_pairs={{0,4},{4,0},{8,12},{12,8},{16,20},{20,16},{24,28},{28,24},{1,5},{5... | collective-permute-start | bytes 3145736 | tf_op jit(solution)/shard_map/ppermute | solution.py:8
  218.7 249.6 %all-gather.9.cloned.1.call-start = ((), (), s32[]{:S(2)}) async-start(), calls=%async_computation.4 | async-start | bytes 2621440 | tf_op jit(solution)/shard_map/all_gather | solution.py:65
  274.7 4.2 copy-start.7
  274.7 5.5 copy-start.18
  280.7 4.0 copy-start.9
  294.8 1.0 copy-start.12
  307.7 61.3 %copy-start.3 = (f32[512,1024]{1,0:T(8,128)S(1)}, f32[512,1024]{1,0:T(8,128)}, u32[]{:S(2)}) copy-start(f32[512,1024]{1,0:T(8,128)} %all-gather.7.cloned.1.call-done) | copy-start | bytes 6291460
  370.1 25.5 %collective-permute-start.1 = (f32[256,1024]{1,0:T(8,128)}, f32[256,1024]{1,0:T(8,128)S(1)}, u32[]{:S(2)}, u32[]{:S(2)}) collective-permute-start(f32[256,1024]{1,0:T(8,128)} %constant_dynamic-slice_fusion.5), channel_id=1, source_target_pairs={{0,8},{4,12},{8,0},{12,4},{16,24},{20,28},{24,16},{28,20},{1,9},{5... | collective-permute-start | bytes 3145736 | tf_op jit(solution)/shard_map/ppermute | solution.py:8
  390.6 4.9 copy-start.4
  397.3 57.5 %copy-start.8 = (f32[512,512]{1,0:T(8,128)S(1)}, f32[512,512]{1,0:T(8,128)}, u32[]{:S(2)}) copy-start(f32[512,512]{1,0:T(8,128)} %fusion.36) | copy-start | bytes 3145732
  399.4 274.1 %all-gather.11.cloned.1.call-start = ((), (), s32[]{:S(2)}) async-start(), calls=%async_computation.5 | async-start | bytes 2621440 | tf_op jit(solution)/shard_map/all_gather | solution.py:65
  454.8 5.2 copy-start.19
  460.4 4.1 copy-start.5
  476.8 1.0 copy-start.13
  549.7 49.3 %collective-permute-start.2 = (f32[256,1024]{1,0:T(8,128)}, f32[256,1024]{1,0:T(8,128)}, u32[]{:S(2)}, u32[]{:S(2)}) collective-permute-start(f32[256,1024]{1,0:T(8,128)} %constant_dynamic-slice_fusion.4), channel_id=1, source_target_pairs={{0,16},{4,20},{8,24},{12,28},{16,0},{20,4},{24,8},{28,12},{1,17},{... | collective-permute-start | bytes 3145736 | tf_op jit(solution)/shard_map/ppermute | solution.py:8
  660.0 5.2 copy-start.20
  665.6 4.1 copy-start.6
  684.0 1.0 copy-start.14
  828.3 4.0 copy-start.10
  832.3 3.0 copy-start.15
  832.3 3.0 copy-start.16
  832.3 3.0 copy-start.17
  834.3 2.6 copy-start.1
Sparse Core Ops, SparseCore 0:
  16.0 55.3 reduce-scatter.1
  74.7 35.1 all-gather.4
  218.8 37.0 all-gather.6
  399.5 36.2 all-gather.8
  604.1 35.8 all-gather.10
where the time goes:
time: 852 us; the launch traced here: 844 us
  other arithmetic  510 us (60%)
  waiting for transfers between devices  119 us (14%)
  matrix products  105 us (12%)
  local copies, waits for them, and re-layouts  80.1 us (9%)
  between operations  25.9 us (3%)
    another operation x56, other arithmetic, basis_from(): factor = jnp.linalg.cholesky(gram)  326 us
    another operation x9, other arithmetic, basis_from(): jax.scipy.linalg.solve_triangular(factor, identity, lower=True)  169 us
    another operation x53, local copies, waits for them, and re-layouts, basis_from(): jax.scipy.linalg.solve_triangular(factor, identity, lower=True)  55.8 us
    reduce_scatter x1, waiting for transfers between devices, on_device(): lax.psum_scatter(jnp.dot(front_rows, sample_matrix, preferred_element_typ...  54.5 us
    all_gather x4, waiting for transfers between devices, on_device(): skeleton_t = lax.all_gather(picked, 'grp', axis=0, tiled=True)  34.1 us
    dot_general x8, matrix products, contract_last(): lax.dot_general(left_side, right_side, (((1,), (1,)), ((), ())), precisio...  30.7 us
    ppermute x3, waiting for transfers between devices, from_partner(): lax.ppermute(x, axis, [(i, i ^ 1 << bit) for i in range(lax.axis_size(axi...  30.4 us
    another operation x28, matrix products, basis_from(): jax.scipy.linalg.solve_triangular(factor, identity, lower=True)  29.2 us
  transfers between devices with their start and end apart: 8, of which 4 were waited for; matrix products, arithmetic and copies ran while one was open for 31% of the time, Pallas kernels for 0%

commit v1 on v0

v1 whole, which is shorter than its diff:
```python
import functools

import jax
import jax.numpy as jnp
from jax import lax
from jax.experimental import pallas as pl
from jax.experimental.pallas import tpu as pltpu
from jax.sharding import PartitionSpec as P

COARSE_CAP = 24
FINE_CAP = 6
COARSE_GOAL = 1e-2
FINE_GOAL = 1e-6


def from_partner(x, axis, mask):
    return lax.ppermute(x, axis, [(i, i ^ mask) for i in range(lax.axis_size(axis))])


def halves(x):
    high = x.astype(jnp.bfloat16)
    return high, (x - high.astype(jnp.float32)).astype(jnp.bfloat16)


def mul(a, b):
    return jnp.dot(a, b, preferred_element_type=jnp.float32)


def mul_t(a, b):
    return lax.dot_general(
        a, b, (((1,), (1,)), ((), ())), preferred_element_type=jnp.float32
    )


def inverse_kernel(skeleton_ref, out_ref, scaled, high, low, inv, swept):
    size = out_ref.shape[0]
    rows = lax.broadcasted_iota(jnp.int32, (size, size), 0)
    lanes = lax.broadcasted_iota(jnp.int32, (size, size), 1)
    diagonal = rows == lanes
    q_high, q_low = halves(skeleton_ref[...])
    gram = mul_t(q_high, q_high) + (mul_t(q_high, q_low) + mul_t(q_low, q_high))
    only = jnp.where(diagonal, gram, 0.0)
    by_lane = lax.rsqrt(jnp.sum(only, axis=0, keepdims=True))
    by_row = lax.rsqrt(jnp.sum(only, axis=1, keepdims=True))
    matrix = gram * by_lane * by_row
    scaled[...] = matrix
    m_high, m_low = halves(matrix)
    high[...] = m_high
    low[...] = m_low
    start = 1.0 / jnp.max(jnp.sum(jnp.abs(matrix), axis=0, keepdims=True))
    inv[...] = jnp.where(diagonal, 2.0 * start, 0.0) - (start * start) * matrix

    def coarse(carry):
        step, _ = carry
        now = inv[...]
        now_high = now.astype(jnp.bfloat16)
        gap = jnp.where(diagonal, 1.0, 0.0) - mul(high[...], now_high)
        inv[...] = now + mul(now_high, gap.astype(jnp.bfloat16))
        return step + 1, jnp.sum(gap * gap)

    def coarse_more(carry):
        step, error = carry
        return (step < COARSE_CAP) & (error > COARSE_GOAL)

    lax.while_loop(coarse_more, coarse, (jnp.int32(0), jnp.float32(1e9)))

    def fine(carry):
        step, _ = carry
        now = inv[...]
        now_high, now_low = halves(now)
        product = mul(high[...], now_high) + (
            mul(low[...], now_high) + mul(high[...], now_low)
        )
        gap = jnp.where(diagonal, 1.0, 0.0) - product
        inv[...] = now + mul(now_high, gap.astype(jnp.bfloat16))
        return step + 1, jnp.sum(gap * gap)

    def fine_more(carry):
        step, error = carry
        return (step < FINE_CAP) & (error > FINE_GOAL)

    _, last = lax.while_loop(fine_more, fine, (jnp.int32(0), jnp.float32(1e9)))
    good = last <= FINE_GOAL

    @pl.when(good)
    def _():
        out_ref[...] = inv[...] * by_lane * by_row

    @pl.when(jnp.logical_not(good))
    def _():
        swept[...] = scaled[...]

        def sweep(k, carry):
            now = swept[...]
            row = jnp.sum(jnp.where(rows == k, now, 0.0), axis=0, keepdims=True)
            col = jnp.sum(jnp.where(lanes == k, now, 0.0), axis=1, keepdims=True)
            pivot = jnp.sum(
                jnp.where(lanes[:1] == k, row, 0.0), axis=1, keepdims=True
            )
            over = 1.0 / pivot
            updated = now - (col * over) * row
            updated = jnp.where(rows == k, row * over, updated)
            updated = jnp.where(lanes == k, col * over, updated)
            swept[...] = jnp.where((rows == k) & (lanes == k), -over, updated)
            return carry

        lax.fori_loop(0, size, sweep, 0)
        out_ref[...] = -swept[...] * by_lane * by_row


def gram_inverse(skeleton_t):
    size, depth = skeleton_t.shape
    return pl.pallas_call(
        inverse_kernel,
        out_shape=jax.ShapeDtypeStruct((size, size), jnp.float32),
        in_specs=[pl.BlockSpec(memory_space=pltpu.VMEM)],
        out_specs=pl.BlockSpec(memory_space=pltpu.VMEM),
        scratch_shapes=[
            pltpu.VMEM((size, size), jnp.float32),
            pltpu.VMEM((size, size), jnp.bfloat16),
            pltpu.VMEM((size, size), jnp.bfloat16),
            pltpu.VMEM((size, size), jnp.float32),
            pltpu.VMEM((size, size), jnp.float32),
        ],
        compiler_params=pltpu.CompilerParams(vmem_limit_bytes=40 * 1024 * 1024),
        cost_estimate=pl.CostEstimate(
            flops=2 * size * size * (3 * depth + 36 * size),
            bytes_accessed=4 * size * (size + depth),
            transcendentals=0,
        ),
        name="gram_inverse",
    )(skeleton_t)


def apply_basis(row_block, skeleton_t, inverse):
    cross = lax.dot_general(
        row_block,
        skeleton_t,
        (((1,), (1,)), ((), ())),
        precision=lax.Precision.HIGH,
        preferred_element_type=jnp.float32,
    )
    return jnp.dot(
        cross,
        inverse,
        precision=lax.Precision.HIGH,
        preferred_element_type=jnp.float32,
    )


def take_rows(x, index):
    return x.at[index].get(mode="promise_in_bounds")


def on_device(front_rows, sample_matrix, pivots):
    leaf_count = lax.axis_size("leaf")
    grp_count = lax.axis_size("grp")
    merges = leaf_count.bit_length() - 1
    leaf_index = lax.axis_index("leaf")
    grp_index = lax.axis_index("grp")
    node_rows = front_rows.shape[0]
    rank_size = pivots.shape[1]
    cols_dev = sample_matrix.shape[1] // grp_count
    rows_dev = node_rows // grp_count
    piv_dev = rank_size // grp_count
    half = rank_size // 2
    row_block = lax.psum_scatter(
        jnp.dot(front_rows, sample_matrix, preferred_element_type=jnp.float32),
        "grp",
        scatter_dimension=0,
        tiled=True,
    )

    def node_pivots(level):
        offset = 2 * leaf_count - (2 * leaf_count >> level)
        return lax.dynamic_index_in_dim(
            pivots, offset + (leaf_index >> level), 0, keepdims=False
        )

    local = lax.dynamic_slice_in_dim(node_pivots(0), grp_index * piv_dev, piv_dev)
    picked = take_rows(row_block, local - grp_index * rows_dev)
    skeletons = [lax.all_gather(picked, "grp", axis=0, tiled=True)]
    blocks = [row_block]
    wanted_side = grp_index // (grp_count // 2)
    for level in range(1, merges + 1):
        below = skeletons[-1]
        bit = level - 1
        side = (leaf_index >> bit) % 2
        mine = lax.dynamic_slice_in_dim(node_pivots(level), side * half, half)
        mine = take_rows(below, mine - side * rank_size)
        other = from_partner(mine, "leaf", 1 << bit)
        upper = jnp.where(side == 0, mine, other)
        lower = jnp.where(side == 0, other, mine)
        skeletons.append(jnp.concatenate([upper, lower], axis=0))
        piece = lax.dynamic_slice_in_dim(
            below, grp_index % (grp_count // 2) * rows_dev, rows_dev, 0
        )
        partner = from_partner(piece, "leaf", 1 << bit)
        blocks.append(jnp.where(side == wanted_side, piece, partner))
    collected = [
        apply_basis(block, skeleton, gram_inverse(skeleton))
        for block, skeleton in zip(blocks, skeletons)
    ]
    top = lax.dynamic_slice_in_dim(skeletons[-1], grp_index * cols_dev, cols_dev, 1).T
    return (jnp.stack(collected)[:, None], top)


def solution(mesh):
    placed = (P("leaf", "grp"), P("grp", None), P())
    return jax.shard_map(
        on_device,
        mesh=mesh,
        in_specs=placed,
        out_specs=(P(None, "leaf", "grp", None), P("grp", None)),
        check_vma=False,
    )
```

time: 852 us -> 328 us (0.38)
  other arithmetic: 510 us -> 12.1 us
  Pallas kernels: 0 us -> 103 us
  matrix products: 105 us -> 22.3 us
  local copies, waits for them, and re-layouts: 80.1 us -> 26.1 us
  waiting for transfers between devices: 119 us -> 143 us
  between operations: 25.9 us -> 14.5 us
    another operation x65 -> x0, other arithmetic: 494 us -> none  [the longest x56 326 us: basis_from(): factor = jnp.linalg.cholesky(gram)]
    pallas_call x0 -> x4, Pallas kernels: none -> 103 us  [gram_inverse(): pl.pallas_call(inverse_kernel, out_shape=jax.ShapeDtypeStruct((size, size...]
    another operation x69 -> x0, local copies, waits for them, and re-layouts: 57.4 us -> none  [the longest x53 55.8 us: basis_from(): jax.scipy.linalg.solve_triangular(factor, identity, lower=True)]
    another operation x52 -> x0, matrix products: 53.4 us -> none  [the longest x28 29.2 us: basis_from(): jax.scipy.linalg.solve_triangular(factor, identity, lower=True)]
    dot_general x16 -> x8, matrix products: 45 us -> 15.4 us  [the longest x4 10.5 us: apply_basis(): lax.dot_general(row_block, skeleton_t, (((1,), (1,)), ((), ())), precisio...]
    ppermute x3 -> x6, waiting for transfers between devices: 30.4 us -> 54.5 us  [from_partner(): lax.ppermute(x, axis, [(i, i ^ mask) for i in range(lax.axis_size(axis))])]
    all_gather x4 -> x1, waiting for transfers between devices: 34.1 us -> 34.3 us  [on_device(): skeletons = [lax.all_gather(picked, 'grp', axis=0, tiled=True)]]
  transfers between devices with their start and end apart: 8 -> 8, of which waited for: 4 -> 4; matrix products, arithmetic and copies ran while one was open for 31% -> 11% of each run, Pallas kernels for 0% -> 32%
where the time goes in v1:
time: 328 us; the launch traced here: 327 us
  waiting for transfers between devices  143 us (44%)
  Pallas kernels  103 us (31%)
  local copies, waits for them, and re-layouts  26.1 us (8%)
  matrix products  22.3 us (7%)
  between operations  14.5 us (4%)
  other arithmetic  12.1 us (4%)
  starting transfers between devices  5.54 us (2%)
    pallas_call x4, Pallas kernels, gram_inverse(): pl.pallas_call(inverse_kernel, out_shape=jax.ShapeDtypeStruct((size, size...  103 us
    reduce_scatter x1, waiting for transfers between devices, on_device(): lax.psum_scatter(jnp.dot(front_rows, sample_matrix, preferred_element_typ...  54.6 us
    ppermute x6, waiting for transfers between devices, from_partner(): lax.ppermute(x, axis, [(i, i ^ mask) for i in range(lax.axis_size(axis))])  54.5 us
    all_gather x1, waiting for transfers between devices, on_device(): skeletons = [lax.all_gather(picked, 'grp', axis=0, tiled=True)]  34.3 us
    gather x4, local copies, waits for them, and re-layouts, take_rows(): return x.at[index].get(mode='promise_in_bounds')  15.3 us
    dot_general x4, matrix products, apply_basis(): lax.dot_general(row_block, skeleton_t, (((1,), (1,)), ((), ())), precisio...  10.5 us
    unnamed x43, local copies, waits for them, and re-layouts  8.39 us
    concatenate x5, other arithmetic, on_device(): skeletons.append(jnp.concatenate([upper, lower], axis=0))  7.46 us
  transfers between devices with their start and end apart: 8, of which 4 were waited for; matrix products, arithmetic and copies ran while one was open for 11% of the time, Pallas kernels for 32%

profile of v1, /device:TPU:0, one launch (start us, length us, event | category | flops | bytes accessed | tf_op | source)
XLA Modules:
  0.0 326.8 jit_solution(15301624304292268579)
XLA Ops:
  7.2 1.8 copy-done
  9.1 6.8 %fusion.14 = f32[1024,1024]{1,0:T(8,128)} fusion(bf16[1024,1536]{1,0:T(8,128)(2,1)S(1)} %copy-done, bf16[1536,1024]{1,0:T(8,128)(2,1)} %param.4), kind=kOutput, calls=%fused_computation.47 | convolution fusion | flops 3221225472 | bytes 10485760 | tf_op jit(solution)/shard_map/dot_general | solution.py:168
  16.0 0.8 fusion.13
  16.8 54.6 %reduce-scatter.2.cloned.1.call-done = f32[256,1024]{1,0:T(8,128)} async-done(((f32[1024,1024]{1,0:T(8,128)}), f32[256,1024]{1,0:T(8,128)}) %reduce-scatter.2.cloned.1.call-update) | async-done | bytes 1048592 | tf_op jit(solution)/shard_map/reduce_scatter | solution.py:167
  71.4 3.0 gather_fusion
  74.5 0.9 compare_select_fusion
  75.5 34.3 %all-gather.3.cloned.1.call-done.skeleton_ref = f32[512,1024]{1,0:T(8,128)} async-done(((f32[128,1024]{1,0:T(8,128)}), f32[512,1024]{1,0:T(8,128)}) %all-gather.3.cloned.1.call-update) | async-done | bytes 2097168 | tf_op jit(solution)/shard_map/all_gather | solution.py:182
  109.8 2.4 constant_dynamic-slice_fusion
  112.2 4.1 %gather_fusion.1 = f32[256,1024]{1,0:T(8,128)} fusion(f32[512,1024]{1,0:T(8,128)} %all-gather.3.cloned.1.call-done.skeleton_ref, s32[1024]{0:T(1024)S(1)} %pad_clamp_fusion.2), kind=kCustom, calls=%fused_computation.1 | custom fusion | bytes 2098176 | tf_op jit(solution)/shard_map/gather | solution.py:152
  116.3 0.5 collective-permute-start.1
  116.8 3.1 fusion.15
  119.8 25.8 %gram_inverse.4 = f32[512,512]{1,0:T(8,128)S(1)} custom-call(f32[512,1024]{1,0:T(8,128)S(1)} %copy-done.1), custom_call_target="tpu_custom_call" | custom-call | flops 11274289152 | bytes 3145728 | tf_op jit(solution)/shard_map/gram_inverse/pallas_call | solution.py:113
  145.6 1.4 convolution_bitcast_fusion.3
  147.1 0.2 broadcast_select_fusion.5
  147.3 1.5 fusion.1
  148.8 0.1 copy-done.7
  148.9 1.5 pad_maximum_fusion.skeleton_ref
  150.3 4.1 %gather_fusion.2 = f32[256,1024]{1,0:T(8,128)} fusion(f32[512,1024]{1,0:T(8,128)} %pad_maximum_fusion.skeleton_ref, s32[1024]{0:T(1024)S(1)} %pad_clamp_fusion.1), kind=kCustom, calls=%fused_computation.2 | custom fusion | bytes 2098176 | tf_op jit(solution)/shard_map/gather | solution.py:152
  154.4 1.5 collective-permute-start.3
  155.9 0.5 collective-permute-start.2
  156.5 1.6 copy-done.3
  158.1 25.8 %gram_inverse.5 = f32[512,512]{1,0:T(8,128)S(1)} custom-call(f32[512,1024]{1,0:T(8,128)S(1)} %copy-done.3), custom_call_target="tpu_custom_call" | custom-call | flops 11274289152 | bytes 3145728 | tf_op jit(solution)/shard_map/gram_inverse/pallas_call | solution.py:113
  183.9 2.3 fusion.6
  186.2 1.5 convolution_bitcast_fusion.2
  187.7 0.2 broadcast_select_fusion.2
  187.9 1.5 fusion
  189.4 2.4 collective-permute-start.4
  191.8 1.5 pad_maximum_fusion.1.skeleton_ref
  193.3 4.1 %gather_fusion.3 = f32[256,1024]{1,0:T(8,128)} fusion(f32[512,1024]{1,0:T(8,128)} %pad_maximum_fusion.1.skeleton_ref, s32[1024]{0:T(1024)S(1)} %pad_clamp_fusion), kind=kCustom, calls=%fused_computation.3 | custom fusion | bytes 2098176 | tf_op jit(solution)/shard_map/gather | solution.py:152
  197.4 0.5 collective-permute-start.5
  197.8 16.0 %collective-permute-done.2 = f32[256,1024]{1,0:T(8,128)} collective-permute-done((f32[256,1024]{1,0:T(8,128)}, f32[256,1024]{1,0:T(8,128)}, u32[]{:S(2)}, u32[]{:S(2)}) %collective-permute-start.2) | collective-permute-done | bytes 1048608 | tf_op jit(solution)/shard_map/ppermute | solution.py:17
  213.9 2.9 fusion.4
  216.8 25.8 %gram_inverse.6 = f32[512,512]{1,0:T(8,128)S(1)} custom-call(f32[512,1024]{1,0:T(8,128)S(1)} %copy-done.2), custom_call_target="tpu_custom_call" | custom-call | flops 11274289152 | bytes 3145728 | tf_op jit(solution)/shard_map/gram_inverse/pallas_call | solution.py:113
  242.6 1.4 convolution_bitcast_fusion.1
  244.1 38.4 %collective-permute-done.5 = f32[256,1024]{1,0:T(8,128)S(1)} collective-permute-done((f32[256,1024]{1,0:T(8,128)}, f32[256,1024]{1,0:T(8,128)S(1)}, u32[]{:S(2)}, u32[]{:S(2)}) %collective-permute-start.5) | collective-permute-done | bytes 1048608 | tf_op jit(solution)/shard_map/ppermute | solution.py:17
  282.5 0.2 broadcast_select_fusion.1
  282.7 1.6 pad_maximum_fusion.2.skeleton_ref
  284.3 0.4 copy-done.13
  284.7 0.9 fusion.9
  285.6 2.0 copy.8
  287.6 1.6 copy-done.4
  289.2 25.6 %gram_inverse.7 = f32[512,512]{1,0:T(8,128)S(1)} custom-call(f32[512,1024]{1,0:T(8,128)S(1)} %copy-done.4), custom_call_target="tpu_custom_call" | custom-call | flops 11274289152 | bytes 3145728 | tf_op jit(solution)/shard_map/gram_inverse/pallas_call | solution.py:113
  314.9 2.3 fusion.2
  317.2 0.6 convolution_bitcast_fusion
  317.8 0.4 copy-done.18
  318.2 0.2 copy-done.19
  318.4 0.2 copy-done.20
  318.5 1.5 maximum_bitcast_fusion
  (47 shorter events, 0.3 us)
Async XLA Ops:
  7.2 1.9 copy-start
  7.2 64.2 %reduce-scatter.2.cloned.1.call-start = ((), (), s32[]{:S(2)}) async-start(), calls=%async_computation.1 | async-start | bytes 5242880 | tf_op jit(solution)/shard_map/reduce_scatter | solution.py:167
  15.9 93.9 %all-gather.3.cloned.1.call-start = ((), (), s32[]{:S(2)}) async-start(), calls=%async_computation.2 | async-start | bytes 2621440 | tf_op jit(solution)/shard_map/all_gather | solution.py:182
  112.2 71.7 %collective-permute-start = (f32[256,1024]{1,0:T(8,128)}, f32[256,1024]{1,0:T(8,128)}, u32[]{:S(2)}, u32[]{:S(2)}) collective-permute-start(f32[256,1024]{1,0:T(8,128)} %constant_dynamic-slice_fusion), channel_id=1, source_target_pairs={{0,4},{4,0},{8,12},{12,8},{16,20},{20,16},{24,28},{28,24},{1,5},{5... | collective-permute-start | bytes 3145736 | tf_op jit(solution)/shard_map/ppermute | solution.py:17
  116.3 3.6 %copy-start.1 = (f32[512,1024]{1,0:T(8,128)S(1)}, f32[512,1024]{1,0:T(8,128)}, u32[]{:S(2)}) copy-start(f32[512,1024]{1,0:T(8,128)} %all-gather.3.cloned.1.call-done.skeleton_ref) | copy-start | bytes 6291460
  116.3 30.8 %collective-permute-start.1 = (f32[256,1024]{1,0:T(8,128)}, f32[256,1024]{1,0:T(8,128)S(1)}, u32[]{:S(2)}, u32[]{:S(2)}) collective-permute-start(f32[256,1024]{1,0:T(8,128)} %gather_fusion.1), channel_id=1, source_target_pairs={{0,4},{4,0},{8,12},{12,8},{16,20},{20,16},{24,28},{28,24},{1,5},{5... | collective-permute-start | bytes 3145736 | tf_op jit(solution)/shard_map/ppermute | solution.py:17
  145.6 1.5 copy-start.17
  147.3 1.5 copy-start.5
  147.3 1.6 copy-start.7
  154.4 33.2 %collective-permute-start.3 = (f32[256,1024]{1,0:T(8,128)}, f32[256,1024]{1,0:T(8,128)S(1)}, u32[]{:S(2)}, u32[]{:S(2)}) collective-permute-start(f32[256,1024]{1,0:T(8,128)} %gather_fusion.2), channel_id=1, source_target_pairs={{0,8},{4,12},{8,0},{12,4},{16,24},{20,28},{24,16},{28,20},{1,9},{5... | collective-permute-start | bytes 3145736 | tf_op jit(solution)/shard_map/ppermute | solution.py:17
  155.9 57.9 %collective-permute-start.2 = (f32[256,1024]{1,0:T(8,128)}, f32[256,1024]{1,0:T(8,128)}, u32[]{:S(2)}, u32[]{:S(2)}) collective-permute-start(f32[256,1024]{1,0:T(8,128)} %fusion.1), channel_id=1, source_target_pairs={{0,8},{4,12},{8,0},{12,4},{16,24},{20,28},{24,16},{28,20},{1,9},{5... | collective-permute-start | bytes 3145736 | tf_op jit(solution)/shard_map/ppermute | solution.py:17
  156.5 1.6 copy-start.3
  158.1 25.8 %copy-start.6 = (f32[256,1024]{1,0:T(8,128)S(1)}, f32[256,1024]{1,0:T(8,128)}, u32[]{:S(2)}) copy-start(f32[256,1024]{1,0:T(8,128)} %copy-done.5) | copy-start | bytes 3145732
  158.1 25.8 %copy-start.8 = (f32[256,1024]{1,0:T(8,128)S(1)}, f32[256,1024]{1,0:T(8,128)}, u32[]{:S(2)}) copy-start(f32[256,1024]{1,0:T(8,128)} %copy-done.7) | copy-start | bytes 3145732
  186.2 1.5 copy-start.15
  187.9 4.0 %copy-start.9 = (f32[256,1024]{1,0:T(8,128)}, f32[256,1024]{1,0:T(8,128)S(1)}, u32[]{:S(2)}) copy-start(f32[256,1024]{1,0:T(8,128)S(1)} %get-tuple-element.8) | copy-start | bytes 3145732
  187.9 4.0 %copy-start.10 = (f32[256,1024]{1,0:T(8,128)}, f32[256,1024]{1,0:T(8,128)S(1)}, u32[]{:S(2)}) copy-start(f32[256,1024]{1,0:T(8,128)S(1)} %get-tuple-element.9) | copy-start | bytes 3145732
  189.4 125.5 %collective-permute-start.4 = (f32[256,1024]{1,0:T(8,128)}, f32[256,1024]{1,0:T(8,128)}, u32[]{:S(2)}, u32[]{:S(2)}) collective-permute-start(f32[256,1024]{1,0:T(8,128)} %fusion), channel_id=1, source_target_pairs={{0,16},{4,20},{8,24},{12,28},{16,0},{20,4},{24,8},{28,12},{1,17},{... | collective-permute-start | bytes 3145736 | tf_op jit(solution)/shard_map/ppermute | solution.py:17
  197.3 19.4 %copy-start.2 = (f32[512,1024]{1,0:T(8,128)S(1)}, f32[512,1024]{1,0:T(8,128)}, u32[]{:S(2)}) copy-start(f32[512,1024]{1,0:T(8,128)} %pad_maximum_fusion.1.skeleton_ref) | copy-start | bytes 6291460
  197.4 85.1 %collective-permute-start.5 = (f32[256,1024]{1,0:T(8,128)}, f32[256,1024]{1,0:T(8,128)S(1)}, u32[]{:S(2)}, u32[]{:S(2)}) collective-permute-start(f32[256,1024]{1,0:T(8,128)} %gather_fusion.3), channel_id=1, source_target_pairs={{0,16},{4,20},{8,24},{12,28},{16,0},{20,4},{24,8},{28,12},{1,17},{... | collective-permute-start | bytes 3145736 | tf_op jit(solution)/shard_map/ppermute | solution.py:17
  242.6 39.9 %copy-start.16 = (f32[256,1024]{1,0:T(8,128)S(1)}, f32[256,1024]{1,0:T(8,128)}, u32[]{:S(2)}) copy-start(f32[256,1024]{1,0:T(8,128)} %gather_fusion.3) | copy-start | bytes 3145732
  282.7 1.6 copy-start.11
  282.7 2.0 copy-start.13
  287.6 1.6 copy-start.4
  289.2 25.6 %copy-start.12 = (f32[256,1024]{1,0:T(8,128)S(1)}, f32[256,1024]{1,0:T(8,128)}, u32[]{:S(2)}) copy-start(f32[256,1024]{1,0:T(8,128)} %copy-done.11) | copy-start | bytes 3145732
  289.2 25.6 %copy-start.14 = (f32[256,1024]{1,0:T(8,128)S(1)}, f32[256,1024]{1,0:T(8,128)}, u32[]{:S(2)}) copy-start(f32[256,1024]{1,0:T(8,128)} %copy-done.13) | copy-start | bytes 3145732
  317.2 1.0 copy-start.18
  317.2 1.2 copy-start.19
  317.2 1.3 copy-start.20
Sparse Core Ops, SparseCore 0:
  16.0 55.3 reduce-scatter.1
  74.6 35.1 all-gather.2
